TPU v7x, 32 devices: a whole 2x2x4 slice. The times are simulated.
32 devices in a mesh: dp: 2 (over core), mp: 16 (over z, y, x).
Axes of the slice: x: 2, y: 2, z: 4, core: 2. Of those that a mesh axis runs over, the one named last changes fastest.
Arguments:
- tokens: bfloat16 [512, 2048], P('dp', 'mp'), may hold values from -6 to 6
- gate_weights: bfloat16 [2, 2048, 7168], P(None, None, 'mp'), may hold values from -0.125 to 0.125
- up_weights: bfloat16 [2, 2048, 7168], P(None, None, 'mp'), may hold values from -0.125 to 0.125
- down_weights: bfloat16 [2, 7168, 2048], P(None, 'mp'), may hold values from -0.0625 to 0.0625
- rhs_gate: float32 [2, 2048, 7168], P(None, 'dp', 'mp'), may hold values from -6 to 6
- rhs_up: float32 [2, 2048, 7168], P(None, 'dp', 'mp'), may hold values from -6 to 6
- rhs_down: float32 [2, 7168, 2048], P(None, 'mp', 'dp'), may hold values from -6 to 6
- damping: float32 [1], replicated, may hold values from 0.5 to 2
Outputs:
- step_gate: float32 [2, 2048, 7168], P(None, 'dp', 'mp')
- step_up: float32 [2, 2048, 7168], P(None, 'dp', 'mp')
- step_down: float32 [2, 7168, 2048], P(None, 'mp', 'dp')
- next_gate: float32 [2, 2048, 7168], P(None, 'dp', 'mp')
- next_up: float32 [2, 2048, 7168], P(None, 'dp', 'mp')
- next_down: float32 [2, 7168, 2048], P(None, 'mp', 'dp')
All inputs are finite; a program needn't handle non-finite values.
Results may differ from a plain program's by a relative error of at most 0.007.
Values may be sent and summed in bfloat16 or wider, within the bound.
A program may use at most 128 MiB of HBM per device.

v0:
```python
import jax
import jax.numpy as jnp
from jax import lax
from jax.sharding import PartitionSpec as P

ITERS = 1


def silu_terms(value):
    sigmoid_value = jax.nn.sigmoid(value)
    return (value * sigmoid_value, sigmoid_value * (1.0 + value * (1.0 - sigmoid_value)))


def matmul(left, right):
    return jnp.dot(left, right, preferred_element_type=jnp.float32)


def rows_product(left, right):
    return lax.dot_general(
        left, right, (((0,), (0,)), ((), ())), preferred_element_type=jnp.float32
    )


def against(left, right):
    return lax.dot_general(
        left, right, (((1,), (1,)), ((), ())), preferred_element_type=jnp.float32
    )


def local_inner(first, second):
    return (
        jnp.sum(first[0] * second[0])
        + jnp.sum(first[1] * second[1])
        + jnp.sum(first[2] * second[2])
    )


def finish_first(partial_value, whole_add):
    summed = lax.psum(partial_value, "mp")
    if whole_add is not None:
        summed = summed + whole_add.astype(jnp.float32)
    return summed.astype(jnp.bfloat16)


def body(tokens, gate_weights, up_weights, down_weights, rhs_gate, rhs_up, rhs_down, damping):
    share = tokens.shape[1]
    offset = lax.axis_index("mp") * share
    total_tokens = tokens.shape[0] * lax.axis_size("dp")
    tokens_whole = lax.all_gather(tokens, "mp", axis=1, tiled=True)
    gate_one = matmul(tokens_whole, gate_weights[0])
    up_one = matmul(tokens_whole, up_weights[0])
    active_one, slope_one = silu_terms(gate_one)
    hidden_one = (active_one * up_one).astype(jnp.bfloat16)
    layer_one = finish_first(matmul(hidden_one, down_weights[0]), tokens_whole)
    gate_two = matmul(layer_one, gate_weights[1])
    up_two = matmul(layer_one, up_weights[1])
    active_two, slope_two = silu_terms(gate_two)
    hidden_two = (active_two * up_two).astype(jnp.bfloat16)

    def curvature(vectors):
        tangent_gate, tangent_up, tangent_down = (
            lax.all_gather(vectors[0].astype(jnp.bfloat16), "dp", axis=1, tiled=True),
            lax.all_gather(vectors[1].astype(jnp.bfloat16), "dp", axis=1, tiled=True),
            lax.all_gather(vectors[2].astype(jnp.bfloat16), "dp", axis=2, tiled=True),
        )
        tan_gate = matmul(tokens_whole, tangent_gate[0])
        tan_up = matmul(tokens_whole, tangent_up[0])
        tan_hidden = (slope_one * up_one * tan_gate + active_one * tan_up).astype(jnp.bfloat16)
        tan_layer = finish_first(
            matmul(tan_hidden, down_weights[0]) + matmul(hidden_one, tangent_down[0]), None
        )
        tan_gate = matmul(tan_layer, gate_weights[1]) + matmul(layer_one, tangent_gate[1])
        tan_up = matmul(tan_layer, up_weights[1]) + matmul(layer_one, tangent_up[1])
        tan_hidden = (slope_two * up_two * tan_gate + active_two * tan_up).astype(jnp.bfloat16)
        second_partial = matmul(tan_hidden, down_weights[1]) + matmul(hidden_two, tangent_down[1])
        second_summed = lax.psum_scatter(second_partial, "mp", scatter_dimension=1, tiled=True)
        layer_slice = lax.dynamic_slice_in_dim(tan_layer, offset, share, 1)
        cotan_share = (layer_slice.astype(jnp.float32) + second_summed).astype(jnp.bfloat16)
        cotan = lax.all_gather(cotan_share, "mp", axis=1, tiled=True)
        grad_down_two = rows_product(hidden_two, cotan)
        back_hidden = against(cotan, down_weights[1])
        back_gate = (back_hidden * up_two * slope_two).astype(jnp.bfloat16)
        back_up = (back_hidden * active_two).astype(jnp.bfloat16)
        grad_gate_two = rows_product(layer_one, back_gate)
        grad_up_two = rows_product(layer_one, back_up)
        back_partial = against(back_gate, gate_weights[1]) + against(back_up, up_weights[1])
        back_layer = finish_first(back_partial, cotan)
        grad_down_one = rows_product(hidden_one, back_layer)
        back_hidden = against(back_layer, down_weights[0])
        back_gate = (back_hidden * up_one * slope_one).astype(jnp.bfloat16)
        back_up = (back_hidden * active_one).astype(jnp.bfloat16)
        grad_gate_one = rows_product(tokens_whole, back_gate)
        grad_up_one = rows_product(tokens_whole, back_up)
        summed_gate, summed_up, summed_down = (
            lax.psum_scatter(
                jnp.stack([grad_gate_one, grad_gate_two]).astype(jnp.bfloat16),
                "dp",
                scatter_dimension=1,
                tiled=True,
            ).astype(jnp.float32),
            lax.psum_scatter(
                jnp.stack([grad_up_one, grad_up_two]).astype(jnp.bfloat16),
                "dp",
                scatter_dimension=1,
                tiled=True,
            ).astype(jnp.float32),
            lax.psum_scatter(
                jnp.stack([grad_down_one, grad_down_two]).astype(jnp.bfloat16),
                "dp",
                scatter_dimension=2,
                tiled=True,
            ).astype(jnp.float32),
        )
        scale = 1.0 / total_tokens
        return (
            summed_gate * scale + damping[0] * vectors[0],
            summed_up * scale + damping[0] * vectors[1],
            summed_down * scale + damping[0] * vectors[2],
        )

    residual = (rhs_gate, rhs_up, rhs_down)
    direction = residual
    solution = (jnp.zeros_like(rhs_gate), jnp.zeros_like(rhs_up), jnp.zeros_like(rhs_down))
    norm_now = lax.psum(local_inner(residual, residual), ("dp", "mp"))
    for rounds in range(ITERS):
        image = curvature(direction)
        along, crossed, squared = lax.psum(
            (
                local_inner(direction, image),
                local_inner(residual, image),
                local_inner(image, image),
            ),
            ("dp", "mp"),
        )
        alpha = norm_now / along
        solution = tuple((solution[k] + alpha * direction[k] for k in range(3)))
        residual = tuple((residual[k] - alpha * image[k] for k in range(3)))
        norm_next = norm_now - 2.0 * alpha * crossed + alpha * alpha * squared
        direction = tuple((residual[k] + norm_next / norm_now * direction[k] for k in range(3)))
        norm_now = norm_next
    return (solution[0], solution[1], solution[2], direction[0], direction[1], direction[2])


def solution(mesh):
    in_specs = (
        P("dp", "mp"),
        P(None, None, "mp"),
        P(None, None, "mp"),
        P(None, "mp", None),
        P(None, "dp", "mp"),
        P(None, "dp", "mp"),
        P(None, "mp", "dp"),
        P(),
    )
    out_specs = (
        P(None, "dp", "mp"),
        P(None, "dp", "mp"),
        P(None, "mp", "dp"),
        P(None, "dp", "mp"),
        P(None, "dp", "mp"),
        P(None, "mp", "dp"),
    )
    return jax.shard_map(body, mesh=mesh, in_specs=in_specs, out_specs=out_specs, check_vma=False)
```

profile of v0, /device:TPU:0, one launch (start us, length us, event | category | flops | bytes accessed | tf_op | source)
XLA Modules:
  0.0 671.9 jit_solution(4627766731937684603)
XLA Ops:
  7.9 3.6 convert_element_type.67
  11.6 3.6 convert_element_type.66
  15.2 3.6 convert_element_type.70
  18.8 46.0 %all-gather.6.cloned.1.call-done = bf16[256,2048]{1,0:T(8,128)(2,1)} async-done(((bf16[256,128]{1,0:T(8,128)(2,1)}), bf16[256,2048]{1,0:T(8,128)(2,1)}) %all-gather.6.cloned.1.call-update) | async-done | bytes 1048592 | tf_op jit(solution)/shard_map/all_gather | solution.py:49
  64.8 2.6 fusion.33
  67.4 2.4 multiply_convert_fusion.5
  72.3 6.6 all-gather.10.cloned.1.call-done
  78.9 2.2 fusion.65
  81.1 14.0 %all-gather.8.cloned.1.call-done = bf16[2,2048,448]{1,2,0:T(8,128)(2,1)} async-done(((bf16[2,1024,448]{1,2,0:T(8,128)(2,1)}), bf16[2,2048,448]{1,2,0:T(8,128)(2,1)}) %all-gather.8.cloned.1.call-update) | async-done | bytes 3670032 | tf_op jit(solution)/shard_map/all_gather | solution.py:62
  95.1 5.6 fusion.29
  100.8 10.4 %all-gather.12.cloned.1.call-done = bf16[2,448,2048]{2,1,0:T(8,128)(2,1)} async-done(((bf16[2,448,1024]{2,1,0:T(8,128)(2,1)}), bf16[2,448,2048]{2,1,0:T(8,128)(2,1)}) %all-gather.12.cloned.1.call-update) | async-done | bytes 3670032 | tf_op jit(solution)/shard_map/all_gather | solution.py:64
  111.2 2.9 convolution_add_fusion.2
  114.1 112.1 %all-reduce.8 = bf16[256,2048]{1,0:T(8,128)(2,1)} all-reduce(f32[256,2048]{1,0:T(8,128)S(1)} %convolution_add_fusion.2), channel_id=1, replica_groups=mesh['dp'=2,'mp'=16] {'mp'}, use_global_device_ids=true, to_apply=%region_4.0 | all-reduce | flops 524288 | bytes 3145728 | tf_op jit(solution)/shard_map/psum | solution.py:39
  226.1 37.1 %all-reduce.5.cloned.1.call-done = f32[256,2048]{1,0:T(8,128)} async-done(((f32[256,2048]{1,0:T(8,128)}), f32[256,2048]{1,0:T(8,128)}) %all-reduce.5.cloned.1.call-update) | async-done | bytes 2097168 | tf_op jit(solution)/shard_map/psum | solution.py:39
  273.8 6.2 fusion.12
  280.0 4.3 convolution_add_fusion.1
  284.3 80.9 %reduce-scatter.5.cloned.1.call-done = f32[256,128]{1,0:T(8,128)} async-done(((f32[256,2048]{1,0:T(8,128)}), f32[256,128]{1,0:T(8,128)}) %reduce-scatter.5.cloned.1.call-update) | async-done | bytes 131088 | tf_op jit(solution)/shard_map/reduce_scatter | solution.py:76
  366.8 49.5 %all-gather.14.cloned.1.call-done = bf16[256,2048]{1,0:T(8,128)(2,1)} async-done(((bf16[256,128]{1,0:T(8,128)(2,1)}), bf16[256,2048]{1,0:T(8,128)(2,1)}) %all-gather.14.cloned.1.call-update) | async-done | bytes 1048592 | tf_op jit(solution)/shard_map/all_gather | solution.py:79
  416.4 2.9 multiply_convert_fusion.2
  423.7 2.9 fusion.4
  426.6 122.9 %all-reduce.7.cloned.1.call-done = f32[256,2048]{1,0:T(8,128)} async-done(((f32[256,2048]{1,0:T(8,128)}), f32[256,2048]{1,0:T(8,128)}) %all-reduce.7.cloned.1.call-update) | async-done | bytes 2097168 | tf_op jit(solution)/shard_map/psum | solution.py:39
  549.5 3.0 fusion.25
  559.8 2.5 pad_maximum_fusion.1
  564.0 2.4 fusion.2
  569.3 4.4 multiply_reduce_fusion.2
  573.7 9.0 %reduce-scatter.9.cloned.1.call-done = bf16[2,1024,448]{1,2,0:T(8,128)(2,1)} async-done(((bf16[2,2048,448]{1,2,0:T(8,128)(2,1)}), bf16[2,1024,448]{1,2,0:T(8,128)(2,1)}) %reduce-scatter.9.cloned.1.call-update) | async-done | bytes 1835024 | tf_op jit(solution)/shard_map/reduce_scatter | solution.py:101
  582.7 4.4 multiply_reduce_fusion.1
  588.6 10.0 %reduce-scatter.11.cloned.1.call-done = bf16[2,448,1024]{2,1,0:T(8,128)(2,1)} async-done(((bf16[2,448,2048]{2,1,0:T(8,128)(2,1)}), bf16[2,448,1024]{2,1,0:T(8,128)(2,1)}) %reduce-scatter.11.cloned.1.call-update) | async-done | bytes 1835024 | tf_op jit(solution)/shard_map/reduce_scatter | solution.py:107
  598.5 4.4 multiply_reduce_fusion
  607.4 40.6 %all-reduce = (f32[]{:T(128)}, f32[]{:T(128)}, f32[]{:T(128)}) all-reduce(f32[]{:T(128)S(6)} %add.108, f32[]{:T(128)S(6)} %add.128, f32[]{:T(128)S(6)} %add.130), channel_id=1, replica_groups=mesh['dp'=2,'mp'=16] {'dp','mp'}, use_global_device_ids=true, to_apply=%region_3.0 | all-reduce | flops 3 | bytes 24 | tf_op jit(solution)/shard_map/psum | solution.py:124
  652.0 9.2 %multiply_add_fusion.1 = (f32[2,1024,448]{1,2,0:T(8,128)}, f32[2,1024,448]{1,2,0:T(8,128)}, f32[2,1024,448]{1,2,0:T(8,128)}, f32[2,1024,448]{1,2,0:T(8,128)}) fusion(f32[2,1024,448]{1,2,0:T(8,128)} %param.13, bf16[2,1024,448]{1,2,0:T(8,128)(2,1)} %reduce-scatter.9.cloned.1.call-done, f32[]{:T(128)S(6)} %div.17, f32[]{:T(128)S(6)} %div.16, f32[]{:T(128)} %bitcast.123, ...), kind=kLoop, calls=%fused_computation.4 | loop fusion | flops 16515072 | bytes 25690124 | tf_op jit(solution)/shard_map/add | solution.py:139
  661.2 4.1 multiply_add_fusion
  (85 shorter events, 31.2 us)
Async XLA Ops:
  7.2 57.6 %all-gather.6.cloned.1.call-start = ((), (), s32[]{:S(2)}) async-start(), calls=%async_computation.4 | async-start | bytes 1114112 | tf_op jit(solution)/shard_map/all_gather | solution.py:49
  7.9 71.0 %all-gather.10.cloned.1.call-start = ((), (), s32[]{:S(2)}) async-start(), calls=%async_computation.6 | async-start | bytes 5505024 | tf_op jit(solution)/shard_map/all_gather | solution.py:63
  11.5 83.6 %all-gather.8.cloned.1.call-start = ((), (), s32[]{:S(2)}) async-start(), calls=%async_computation.5 | async-start | bytes 5505024 | tf_op jit(solution)/shard_map/all_gather | solution.py:62
  15.2 96.0 %all-gather.12.cloned.1.call-start = ((), (), s32[]{:S(2)}) async-start(), calls=%async_computation.7 | async-start | bytes 5505024 | tf_op jit(solution)/shard_map/all_gather | solution.py:64
  18.8 244.4 %all-reduce.5.cloned.1.call-start = ((), (), s32[]{:S(2)}) async-start(), calls=%async_computation.8 | async-start | bytes 4194304 | tf_op jit(solution)/shard_map/psum | solution.py:39
  64.8 2.6 copy-start.2
  67.4 27.7 %copy-start.8 = (f32[256,448]{0,1:T(8,128)}, f32[256,448]{0,1:T(8,128)S(1)}, u32[]{:S(2)}) copy-start(f32[256,448]{0,1:T(8,128)S(1)} %fusion.33) | copy-start | bytes 1376260
  67.4 2.8 copy-start.7
  69.8 25.3 %copy-start.18 = (f32[256,448]{0,1:T(8,128)}, f32[256,448]{0,1:T(8,128)S(1)}, u32[]{:S(2)}) copy-start(f32[256,448]{0,1:T(8,128)S(1)} %get-tuple-element.27) | copy-start | bytes 1376260
  72.3 293.0 %reduce-scatter.5.cloned.1.call-start = ((), (), s32[]{:S(2)}) async-start(), calls=%async_computation.9 | async-start | bytes 2228224 | tf_op jit(solution)/shard_map/reduce_scatter | solution.py:76
  263.2 2.7 copy-start.14
  263.2 3.8 copy-start.16
  267.0 3.1 copy-start.22
  267.0 2.5 copy-start.20
  267.0 3.1 copy-start.10
  270.1 2.2 copy-start.21
  284.3 132.1 %all-gather.14.cloned.1.call-start = ((), (), s32[]{:S(2)}) async-start(), calls=%async_computation.10 | async-start | bytes 1114112 | tf_op jit(solution)/shard_map/all_gather | solution.py:79
  366.8 182.6 %all-reduce.7.cloned.1.call-start = ((), (), s32[]{:S(2)}) async-start(), calls=%async_computation.11 | async-start | bytes 4194304 | tf_op jit(solution)/shard_map/psum | solution.py:39
  416.4 3.2 copy-start.15
  419.3 1.0 copy-start.12
  419.3 2.3 copy-start.17
  423.6 125.8 %copy-start.1 = (bf16[256,2048]{1,0:T(8,128)(2,1)S(1)}, bf16[256,2048]{1,0:T(8,128)(2,1)}, u32[]{:S(2)}) copy-start(bf16[256,2048]{1,0:T(8,128)(2,1)} %all-gather.14.cloned.1.call-done) | copy-start | bytes 3145732
  423.6 145.7 %reduce-scatter.7.cloned.1.call-start = ((), (), s32[]{:S(2)}) async-start(), calls=%async_computation.12 | async-start | bytes 5505024 | tf_op jit(solution)/shard_map/reduce_scatter | solution.py:95
  549.4 3.8 copy-start.9
  549.4 3.8 copy-start.19
  549.5 4.5 copy-start.4
  556.1 26.6 %reduce-scatter.9.cloned.1.call-start = ((), (), s32[]{:S(2)}) async-start(), calls=%async_computation.13 | async-start | bytes 5505024 | tf_op jit(solution)/shard_map/reduce_scatter | solution.py:101
  562.3 1.0 copy-start.11
  562.4 36.2 %reduce-scatter.11.cloned.1.call-start = ((), (), s32[]{:S(2)}) async-start(), calls=%async_computation.14 | async-start | bytes 5505024 | tf_op jit(solution)/shard_map/reduce_scatter | solution.py:107
  587.2 64.8 %copy-start.3 = (bf16[2,1024,448]{1,2,0:T(8,128)(2,1)S(1)}, bf16[2,1024,448]{1,2,0:T(8,128)(2,1)}, u32[]{:S(2)}) copy-start(bf16[2,1024,448]{1,2,0:T(8,128)(2,1)} %reduce-scatter.7.cloned.1.call-done) | copy-start | bytes 5505028
  652.0 9.2 %copy-start = (f32[2,448,1024]{2,1,0:T(8,128)S(1)}, f32[2,448,1024]{2,1,0:T(8,128)}, u32[]{:S(2)}) copy-start(f32[2,448,1024]{2,1,0:T(8,128)} %param.14) | copy-start | bytes 11010052
  652.0 9.2 %copy-start.5 = (bf16[2,448,1024]{2,1,0:T(8,128)(2,1)S(1)}, bf16[2,448,1024]{2,1,0:T(8,128)(2,1)}, u32[]{:S(2)}) copy-start(bf16[2,448,1024]{2,1,0:T(8,128)(2,1)} %reduce-scatter.11.cloned.1.call-done) | copy-start | bytes 5505028
  (2 other events, 1.8 us)
Sparse Core Ops, SparseCore 0:
  10.7 54.0 all-gather.5
  66.9 11.8 all-gather.9
  81.0 14.0 all-gather.7
  97.1 14.0 all-gather.11
  117.1 146.0 all-reduce.4
  284.4 80.7 reduce-scatter.4
  368.5 47.8 all-gather.13
  423.8 125.6 all-reduce.6
  556.3 10.8 reduce-scatter.6
  569.8 12.9 reduce-scatter.8
  585.6 12.8 reduce-scatter.10
where the time goes:
time: 673 us; the launch traced here: 672 us
  waiting for transfers between devices  387 us (58%)
  blocking collectives  153 us (23%)
  matrix products  52.7 us (8%)
  other arithmetic  47.6 us (7%)
  between operations  24.7 us (4%)
    psum x2, waiting for transfers between devices, finish_first(): summed = lax.psum(partial_value, 'mp')  160 us
    psum x1, blocking collectives, finish_first(): summed = lax.psum(partial_value, 'mp')  112 us
    reduce_scatter x1, waiting for transfers between devices, curvature(): lax.psum_scatter(second_partial, 'mp', scatter_dimension=1, tiled=True)  80.9 us
    all_gather x1, waiting for transfers between devices, curvature(): cotan = lax.all_gather(cotan_share, 'mp', axis=1, tiled=True)  49.5 us
    all_gather x1, waiting for transfers between devices, body(): tokens_whole = lax.all_gather(tokens, 'mp', axis=1, tiled=True)  46 us
    psum x1, blocking collectives, body(): norm_now = lax.psum(local_inner(residual, residual), ('dp', 'mp'))  40.6 us
    dot_general x13, matrix products, matmul(): return jnp.dot(left, right, preferred_element_type=jnp.float32)  34 us
    all_gather x1, waiting for transfers between devices, curvature(): lax.all_gather(vectors[0].astype(jnp.bfloat16), 'dp', axis=1, tiled=True)  14 us
  transfers between devices with their start and end apart: 11, of which 10 were waited for; matrix products, arithmetic and copies ran while one was open for 8% of the time, Pallas kernels for 0%

commit v1 on v0

--- a/solution.py
+++ b/solution.py
@@ -121,7 +121,7 @@
     residual = (rhs_gate, rhs_up, rhs_down)
     direction = residual
     solution = (jnp.zeros_like(rhs_gate), jnp.zeros_like(rhs_up), jnp.zeros_like(rhs_down))
-    norm_now = lax.psum(local_inner(residual, residual), ("dp", "mp"))
+    norm_now = lax.psum(lax.psum(local_inner(residual, residual), "mp"), "dp")
     for rounds in range(ITERS):
         image = curvature(direction)
         along, crossed, squared = lax.psum(

time: 673 us -> 715 us (1.062)
  blocking collectives: 153 us -> 194 us
    psum x1 -> x3, blocking collectives: 40.6 us -> 82.4 us  [the longest x2 45.6 us: body(): norm_now = lax.psum(lax.psum(local_inner(residual, residual), 'mp'), 'dp')]
  transfers between devices with their start and end apart: 11 -> 11, of which waited for: 10 -> 10; matrix products, arithmetic and copies ran while one was open for 8% -> 7% of each run, Pallas kernels for 0% -> 0%
where the time goes in v1:
time: 715 us; the launch traced here: 714 us
  waiting for transfers between devices  387 us (54%)
  blocking collectives  194 us (27%)
  matrix products  52.7 us (7%)
  other arithmetic  47.6 us (7%)
  between operations  24.7 us (3%)
    psum x2, waiting for transfers between devices, finish_first(): summed = lax.psum(partial_value, 'mp')  160 us
    psum x1, blocking collectives, finish_first(): summed = lax.psum(partial_value, 'mp')  112 us
    reduce_scatter x1, waiting for transfers between devices, curvature(): lax.psum_scatter(second_partial, 'mp', scatter_dimension=1, tiled=True)  80.9 us
    all_gather x1, waiting for transfers between devices, curvature(): cotan = lax.all_gather(cotan_share, 'mp', axis=1, tiled=True)  49.5 us
    all_gather x1, waiting for transfers between devices, body(): tokens_whole = lax.all_gather(tokens, 'mp', axis=1, tiled=True)  46 us
    psum x2, blocking collectives, body(): norm_now = lax.psum(lax.psum(local_inner(residual, residual), 'mp'), 'dp')  45.6 us
    psum x1, blocking collectives, body(): lax.psum((local_inner(direction, image), local_inner(residual, image), lo...  36.8 us
    dot_general x13, matrix products, matmul(): return jnp.dot(left, right, preferred_element_type=jnp.float32)  34 us
  transfers between devices with their start and end apart: 11, of which 10 were waited for; matrix products, arithmetic and copies ran while one was open for 7% of the time, Pallas kernels for 0%

profile of v1, /device:TPU:0, one launch (start us, length us, event | category | flops | bytes accessed | tf_op | source)
XLA Modules:
  0.0 713.7 jit_solution(4923316639093777303)
XLA Ops:
  7.9 3.6 convert_element_type.67
  11.6 3.6 convert_element_type.66
  15.2 3.6 convert_element_type.70
  18.8 46.0 %all-gather.6.cloned.1.call-done = bf16[256,2048]{1,0:T(8,128)(2,1)} async-done(((bf16[256,128]{1,0:T(8,128)(2,1)}), bf16[256,2048]{1,0:T(8,128)(2,1)}) %all-gather.6.cloned.1.call-update) | async-done | bytes 1048592 | tf_op jit(solution)/shard_map/all_gather | solution.py:49
  64.8 2.6 fusion.33
  72.3 6.6 all-gather.10.cloned.1.call-done
  81.1 14.0 %all-gather.8.cloned.1.call-done = bf16[2,2048,448]{1,2,0:T(8,128)(2,1)} async-done(((bf16[2,1024,448]{1,2,0:T(8,128)(2,1)}), bf16[2,2048,448]{1,2,0:T(8,128)(2,1)}) %all-gather.8.cloned.1.call-update) | async-done | bytes 3670032 | tf_op jit(solution)/shard_map/all_gather | solution.py:62
  95.1 5.6 fusion.29
  100.8 10.4 %all-gather.12.cloned.1.call-done = bf16[2,448,2048]{2,1,0:T(8,128)(2,1)} async-done(((bf16[2,448,1024]{2,1,0:T(8,128)(2,1)}), bf16[2,448,2048]{2,1,0:T(8,128)(2,1)}) %all-gather.12.cloned.1.call-update) | async-done | bytes 3670032 | tf_op jit(solution)/shard_map/all_gather | solution.py:64
  111.2 2.9 convolution_add_fusion.2
  114.1 112.1 %all-reduce.8 = bf16[256,2048]{1,0:T(8,128)(2,1)} all-reduce(f32[256,2048]{1,0:T(8,128)S(1)} %convolution_add_fusion.2), channel_id=1, replica_groups=mesh['dp'=2,'mp'=16] {'mp'}, use_global_device_ids=true, to_apply=%region_5.0 | all-reduce | flops 524288 | bytes 3145728 | tf_op jit(solution)/shard_map/psum | solution.py:39
  226.1 37.1 %all-reduce.5.cloned.1.call-done = f32[256,2048]{1,0:T(8,128)} async-done(((f32[256,2048]{1,0:T(8,128)}), f32[256,2048]{1,0:T(8,128)}) %all-reduce.5.cloned.1.call-update) | async-done | bytes 2097168 | tf_op jit(solution)/shard_map/psum | solution.py:39
  273.8 6.2 fusion.12
  280.0 4.3 convolution_add_fusion.1
  284.3 80.9 %reduce-scatter.5.cloned.1.call-done = f32[256,128]{1,0:T(8,128)} async-done(((f32[256,2048]{1,0:T(8,128)}), f32[256,128]{1,0:T(8,128)}) %reduce-scatter.5.cloned.1.call-update) | async-done | bytes 131088 | tf_op jit(solution)/shard_map/reduce_scatter | solution.py:76
  366.8 49.5 %all-gather.14.cloned.1.call-done = bf16[256,2048]{1,0:T(8,128)(2,1)} async-done(((bf16[256,128]{1,0:T(8,128)(2,1)}), bf16[256,2048]{1,0:T(8,128)(2,1)}) %all-gather.14.cloned.1.call-update) | async-done | bytes 1048592 | tf_op jit(solution)/shard_map/all_gather | solution.py:79
  416.4 2.9 multiply_convert_fusion.2
  423.7 2.9 fusion.4
  426.6 122.9 %all-reduce.7.cloned.1.call-done = f32[256,2048]{1,0:T(8,128)} async-done(((f32[256,2048]{1,0:T(8,128)}), f32[256,2048]{1,0:T(8,128)}) %all-reduce.7.cloned.1.call-update) | async-done | bytes 2097168 | tf_op jit(solution)/shard_map/psum | solution.py:39
  549.5 3.0 fusion.25
  559.8 2.5 pad_maximum_fusion.1
  564.0 2.4 fusion.2
  569.3 4.4 multiply_reduce_fusion.2
  573.7 9.0 %reduce-scatter.9.cloned.1.call-done = bf16[2,1024,448]{1,2,0:T(8,128)(2,1)} async-done(((bf16[2,2048,448]{1,2,0:T(8,128)(2,1)}), bf16[2,1024,448]{1,2,0:T(8,128)(2,1)}) %reduce-scatter.9.cloned.1.call-update) | async-done | bytes 1835024 | tf_op jit(solution)/shard_map/reduce_scatter | solution.py:101
  582.7 4.4 multiply_reduce_fusion.1
  588.6 9.9 %reduce-scatter.11.cloned.1.call-done = bf16[2,448,1024]{2,1,0:T(8,128)(2,1)} async-done(((bf16[2,448,2048]{2,1,0:T(8,128)(2,1)}), bf16[2,448,1024]{2,1,0:T(8,128)(2,1)}) %reduce-scatter.11.cloned.1.call-update) | async-done | bytes 1835024 | tf_op jit(solution)/shard_map/reduce_scatter | solution.py:107
  598.5 4.4 multiply_reduce_fusion
  603.6 42.6 %psum.52 = f32[]{:T(128)} all-reduce(f32[]{:T(128)S(6)} %add.110), channel_id=1, replica_groups=mesh['dp'=2,'mp'=16] {'mp'}, use_global_device_ids=true, to_apply=%region_3.0 | all-reduce | flops 1 | bytes 8 | tf_op jit(solution)/shard_map/psum | solution.py:124
  650.1 3.0 psum.53
  653.0 36.8 %all-reduce = (f32[]{:T(128)}, f32[]{:T(128)}) all-reduce(f32[]{:T(128)S(6)} %add.130, f32[]{:T(128)S(6)} %add.132), channel_id=1, replica_groups=mesh['dp'=2,'mp'=16] {'dp','mp'}, use_global_device_ids=true, to_apply=%region_15.0 | all-reduce | flops 2 | bytes 16 | tf_op jit(solution)/shard_map/psum | solution.py:127
  693.8 9.2 %multiply_add_fusion.1 = (f32[2,1024,448]{1,2,0:T(8,128)}, f32[2,1024,448]{1,2,0:T(8,128)}, f32[2,1024,448]{1,2,0:T(8,128)}, f32[2,1024,448]{1,2,0:T(8,128)}) fusion(f32[2,1024,448]{1,2,0:T(8,128)} %param.13, bf16[2,1024,448]{1,2,0:T(8,128)(2,1)} %reduce-scatter.9.cloned.1.call-done, f32[]{:T(128)S(6)} %div.17, f32[]{:T(128)S(6)} %div.16, f32[]{:T(128)} %bitcast.123, ...), kind=kLoop, calls=%fused_computation.4 | loop fusion | flops 16515072 | bytes 25690124 | tf_op jit(solution)/shard_map/add | solution.py:139
  703.0 4.1 multiply_add_fusion
  (87 shorter events, 35.8 us)
Async XLA Ops:
  7.2 57.6 %all-gather.6.cloned.1.call-start = ((), (), s32[]{:S(2)}) async-start(), calls=%async_computation.4 | async-start | bytes 1114112 | tf_op jit(solution)/shard_map/all_gather | solution.py:49
  7.9 71.0 %all-gather.10.cloned.1.call-start = ((), (), s32[]{:S(2)}) async-start(), calls=%async_computation.6 | async-start | bytes 5505024 | tf_op jit(solution)/shard_map/all_gather | solution.py:63
  11.5 83.6 %all-gather.8.cloned.1.call-start = ((), (), s32[]{:S(2)}) async-start(), calls=%async_computation.5 | async-start | bytes 5505024 | tf_op jit(solution)/shard_map/all_gather | solution.py:62
  15.2 96.0 %all-gather.12.cloned.1.call-start = ((), (), s32[]{:S(2)}) async-start(), calls=%async_computation.7 | async-start | bytes 5505024 | tf_op jit(solution)/shard_map/all_gather | solution.py:64
  18.8 244.4 %all-reduce.5.cloned.1.call-start = ((), (), s32[]{:S(2)}) async-start(), calls=%async_computation.8 | async-start | bytes 4194304 | tf_op jit(solution)/shard_map/psum | solution.py:39
  64.8 2.6 copy-start.2
  67.4 27.7 %copy-start.8 = (f32[256,448]{0,1:T(8,128)}, f32[256,448]{0,1:T(8,128)S(1)}, u32[]{:S(2)}) copy-start(f32[256,448]{0,1:T(8,128)S(1)} %fusion.33) | copy-start | bytes 1376260
  67.4 2.8 copy-start.7
  69.8 25.3 %copy-start.18 = (f32[256,448]{0,1:T(8,128)}, f32[256,448]{0,1:T(8,128)S(1)}, u32[]{:S(2)}) copy-start(f32[256,448]{0,1:T(8,128)S(1)} %get-tuple-element.26) | copy-start | bytes 1376260
  72.3 293.0 %reduce-scatter.5.cloned.1.call-start = ((), (), s32[]{:S(2)}) async-start(), calls=%async_computation.9 | async-start | bytes 2228224 | tf_op jit(solution)/shard_map/reduce_scatter | solution.py:76
  263.2 2.7 copy-start.14
  263.2 3.8 copy-start.16
  267.0 3.1 copy-start.22
  267.0 2.5 copy-start.20
  267.0 3.1 copy-start.10
  270.1 2.2 copy-start.21
  284.3 132.1 %all-gather.14.cloned.1.call-start = ((), (), s32[]{:S(2)}) async-start(), calls=%async_computation.10 | async-start | bytes 1114112 | tf_op jit(solution)/shard_map/all_gather | solution.py:79
  366.8 182.6 %all-reduce.7.cloned.1.call-start = ((), (), s32[]{:S(2)}) async-start(), calls=%async_computation.11 | async-start | bytes 4194304 | tf_op jit(solution)/shard_map/psum | solution.py:39
  416.4 3.2 copy-start.15
  419.3 1.0 copy-start.12
  419.3 2.3 copy-start.17
  423.6 125.8 %copy-start.1 = (bf16[256,2048]{1,0:T(8,128)(2,1)S(1)}, bf16[256,2048]{1,0:T(8,128)(2,1)}, u32[]{:S(2)}) copy-start(bf16[256,2048]{1,0:T(8,128)(2,1)} %all-gather.14.cloned.1.call-done) | copy-start | bytes 3145732
  423.6 145.7 %reduce-scatter.7.cloned.1.call-start = ((), (), s32[]{:S(2)}) async-start(), calls=%async_computation.12 | async-start | bytes 5505024 | tf_op jit(solution)/shard_map/reduce_scatter | solution.py:95
  549.4 3.8 copy-start.9
  549.4 3.8 copy-start.19
  549.5 4.5 copy-start.4
  556.1 26.6 %reduce-scatter.9.cloned.1.call-start = ((), (), s32[]{:S(2)}) async-start(), calls=%async_computation.13 | async-start | bytes 5505024 | tf_op jit(solution)/shard_map/reduce_scatter | solution.py:101
  562.3 1.0 copy-start.11
  562.4 36.2 %reduce-scatter.11.cloned.1.call-start = ((), (), s32[]{:S(2)}) async-start(), calls=%async_computation.14 | async-start | bytes 5505024 | tf_op jit(solution)/shard_map/reduce_scatter | solution.py:107
  587.2 106.6 %copy-start.3 = (bf16[2,1024,448]{1,2,0:T(8,128)(2,1)S(1)}, bf16[2,1024,448]{1,2,0:T(8,128)(2,1)}, u32[]{:S(2)}) copy-start(bf16[2,1024,448]{1,2,0:T(8,128)(2,1)} %reduce-scatter.7.cloned.1.call-done) | copy-start | bytes 5505028
  693.8 9.2 %copy-start = (f32[2,448,1024]{2,1,0:T(8,128)S(1)}, f32[2,448,1024]{2,1,0:T(8,128)}, u32[]{:S(2)}) copy-start(f32[2,448,1024]{2,1,0:T(8,128)} %param.14) | copy-start | bytes 11010052
  693.8 9.2 %copy-start.5 = (bf16[2,448,1024]{2,1,0:T(8,128)(2,1)S(1)}, bf16[2,448,1024]{2,1,0:T(8,128)(2,1)}, u32[]{:S(2)}) copy-start(bf16[2,448,1024]{2,1,0:T(8,128)(2,1)} %reduce-scatter.11.cloned.1.call-done) | copy-start | bytes 5505028
  (2 other events, 1.8 us)
Sparse Core Ops, SparseCore 0:
  10.7 54.0 all-gather.5
  66.9 11.8 all-gather.9
  81.0 14.0 all-gather.7
  97.1 14.0 all-gather.11
  117.1 146.0 all-reduce.4
  284.4 80.7 reduce-scatter.4
  368.5 47.8 all-gather.13
  423.8 125.6 all-reduce.6
  556.3 10.8 reduce-scatter.6
  569.8 12.9 reduce-scatter.8
  585.6 12.8 reduce-scatter.10
